TPU v7x, 32 devices: a whole 2x2x4 slice. The times are simulated.
32 devices in a mesh: col: 16 (over z, y, x), row: 2 (over core).
Axes of the slice: x: 2, y: 2, z: 4, core: 2. Of those that a mesh axis runs over, the one named last changes fastest.
Arguments:
- gradient: bfloat16 [4096, 16384], P('row', 'col'), may hold values from -120 to 120
- momentum: float32 [4096, 16384], P('row', 'col'), may hold values from -6 to 6
- right_factor: float32 [16384, 256], P(('col', 'row')), may hold values from -0.046875 to 0.046875
Outputs:
- momentum_next: float32 [4096, 16384], P('row', 'col')
- right_next: float32 [16384, 256], P(('col', 'row'))
- update: bfloat16 [4096, 16384], P('row', 'col')
All inputs are finite; a program needn't handle non-finite values.
Results may differ from a plain program's by a relative error of at most 0.0012.
Values sent between devices are 32-bit elements; how exact they have to be, the bound alone decides.
No kernel may reach another device: no remote copies, remote signals or barrier semaphores. Data moves between devices by JAX's collectives and lax.ppermute only.
A program may use at most 64 MiB of HBM per device.

v0:
```python
import math
import jax
import jax.numpy as jnp
from jax import lax
from jax.sharding import PartitionSpec as P

M = 4096
N = 16384
RANK = 256
EPS = 1e-06
FEEDBACK = 0.05


def body(gradient, momentum, right_factor):
    highest = lax.Precision.HIGHEST
    blend = momentum + gradient.astype(jnp.float32)
    right_block = lax.all_gather(right_factor, "row", axis=0, tiled=True)
    contract_rows = (((0,), (0,)), ((), ()))
    partial_value = jnp.dot(
        blend, right_block, precision=highest, preferred_element_type=jnp.float32
    )
    left = lax.psum(partial_value, "col")
    local_gram = lax.dot_general(
        left, left, contract_rows, precision=highest, preferred_element_type=jnp.float32
    )
    gram = lax.psum(local_gram, "row")
    lower = jnp.linalg.cholesky(gram)
    left_orth = jax.scipy.linalg.solve_triangular(lower, left.T, lower=True).T
    right_local = lax.dot_general(
        blend, left_orth, contract_rows, precision=highest, preferred_element_type=jnp.float32
    )
    share = lax.psum_scatter(right_local, "row", scatter_dimension=0, tiled=True)
    squares_right = lax.psum(jnp.sum(share * share, axis=0), ("col", "row"))
    right_norm = jnp.sqrt(squares_right + EPS)
    right_next = share / right_norm[None, :]
    right_whole = lax.all_gather(share, "row", axis=0, tiled=True)
    right_unit = right_whole / right_norm[None, :]
    contract_cols = (((1,), (1,)), ((), ()))
    feedback_term = lax.dot_general(
        left_orth, right_whole, contract_cols, precision=highest, preferred_element_type=jnp.float32
    )
    momentum_next = blend - FEEDBACK * feedback_term
    factor = math.sqrt(M * N / RANK)
    direction = lax.dot_general(
        left_orth, right_unit, contract_cols, precision=highest, preferred_element_type=jnp.float32
    )
    update = (factor * direction).astype(jnp.bfloat16)
    return (momentum_next, right_next, update)


def solution(mesh):
    placed = (P("row", "col"), P("row", "col"), P(("col", "row"), None))
    return jax.shard_map(
        body,
        mesh=mesh,
        in_specs=placed,
        out_specs=(P("row", "col"), P(("col", "row"), None), P("row", "col")),
        check_vma=False,
    )
```

profile of v0, /device:TPU:0, one launch (start us, length us, event | category | flops | bytes accessed | tf_op | source)
XLA Modules:
  0.0 361.9 jit_solution(6752334707807662119)
XLA Ops:
  7.9 13.4 %all-gather.3.cloned.1.call-done = f32[1024,256]{1,0:T(8,128)} async-done(((f32[512,256]{1,0:T(8,128)}), f32[1024,256]{1,0:T(8,128)}) %all-gather.3.cloned.1.call-update) | async-done | bytes 1048592 | tf_op jit(solution)/shard_map/all_gather | solution.py:17
  21.3 11.0 %fusion.1 = f32[2048,256]{1,0:T(8,128)} fusion(f32[1024,256]{1,0:T(8,128)} %all-gather.3.cloned.1.call-done, f32[2048,1024]{1,0:T(8,128)} %param.4, bf16[2048,1024]{1,0:T(8,128)(2,1)} %param.3), kind=kOutput, calls=%fused_computation.6 | convolution fusion | flops 6446645248 | bytes 15728640 | tf_op jit(solution)/shard_map/dot_general | solution.py:19
  32.3 127.9 %all-reduce.4.cloned.1.call-done = f32[2048,256]{1,0:T(8,128)} async-done(((f32[2048,256]{1,0:T(8,128)}), f32[2048,256]{1,0:T(8,128)}) %all-reduce.4.cloned.1.call-update) | async-done | bytes 2097168 | tf_op jit(solution)/shard_map/psum | solution.py:22
  160.2 6.5 %fusion.16 = f32[256,256]{0,1:T(8,128)} fusion(f32[2048,256]{1,0:T(8,128)} %all-reduce.4.cloned.1.call-done), kind=kOutput, calls=%fused_computation.42 | convolution fusion | flops 1610612736 | bytes 2359296 | tf_op jit(solution)/shard_map/dot_general | solution.py:23
  167.3 17.0 %all-reduce.6.cloned.1.call-done = f32[256,256]{0,1:T(8,128)} async-done(((f32[256,256]{0,1:T(8,128)}), f32[256,256]{0,1:T(8,128)}) %all-reduce.6.cloned.1.call-update) | async-done | bytes 262160 | tf_op jit(solution)/shard_map/psum | solution.py:26
  184.4 1.1 copy.7
  185.5 1.0 fusion.6
  186.5 11.7 %cholesky.50 = f32[128,128]{1,0:T(8,128)S(1)} custom-call(f32[128,128]{1,0:T(8,128)S(1)} %cholesky.118), custom_call_target="Cholesky" | custom-call | tf_op jit(solution)/shard_map/jit(cholesky)/cholesky | solution.py:27
  198.2 9.8 %custom-call.15 = f32[1,128,128]{1,2,0:T(8,128)S(1)} custom-call(f32[1,128,128]{2,1,0:T(8,128)S(1)} %get-tuple-element.24), custom_call_target="InvertDiagBlocksLowerTriangular" | custom-call | tf_op jit(solution)/shard_map/jit(cholesky)/cholesky | solution.py:27
  208.5 11.7 %cholesky.105 = f32[128,128]{1,0:T(8,128)S(1)} custom-call(f32[128,128]{1,0:T(8,128)S(1)} %convolution_subtract_fusion.1), custom_call_target="Cholesky" | custom-call | tf_op jit(solution)/shard_map/jit(cholesky)/cholesky | solution.py:27
  222.3 4.2 %while.1 = (s32[]{:T(128)}, f32[256,256]{1,0:T(8,128)S(1)}, s32[2,2]{1,0:T(2,128)S(1)}, f32[2,128,128]{2,1,0:T(8,128)S(1)}, s32[]{:T(128)}) while((s32[]{:T(128)}, f32[256,256]{1,0:T(8,128)S(1)}, s32[2,2]{1,0:T(2,128)S(1)}, f32[2,128,128]{2,1,0:T(8,128)S(1)}, s32[]{:T(128)}) %tuple.27), condition=%wide.while_cond, body=%wide.while_body.sunk | while | flops 2 | bytes 131189 | solution.py:28
  223.1 1.4 bitcast_dynamic-update-slice_fusion.2
  225.1 1.4 bitcast_dynamic-update-slice_fusion.2
  226.5 19.7 %custom-call.16 = f32[2,128,128]{1,2,0:T(8,128)S(1)} custom-call(f32[2,128,128]{2,1,0:T(8,128)S(1)} %get-tuple-element.10), custom_call_target="InvertDiagBlocksLowerTriangular" | custom-call | tf_op jit(solution)/shard_map/jit(_solve_triangular)/triangular_solve | solution.py:28
  246.2 1.1 fusion.2
  247.3 1.8 convolution_subtract_fusion
  249.1 1.1 fusion.8
  250.2 16.6 %fusion = f32[1024,256]{1,0:T(8,128)} fusion(f32[2048,1024]{1,0:T(8,128)} %param.4, bf16[2048,1024]{1,0:T(8,128)(2,1)S(1)} %copy-done, f32[128,2048]{1,0:T(8,128)S(1)} %fusion.8, f32[128,2048]{1,0:T(8,128)S(1)} %fusion.2), kind=kOutput, calls=%fused_computation.5 | convolution fusion | flops 6447169536 | bytes 15728640 | tf_op jit(solution)/shard_map/dot_general | solution.py:29
  266.9 9.7 %reduce-scatter.2.cloned.1.call-done = f32[512,256]{1,0:T(8,128)} async-done(((f32[1024,256]{1,0:T(8,128)}), f32[512,256]{1,0:T(8,128)}) %reduce-scatter.2.cloned.1.call-update) | async-done | bytes 524304 | tf_op jit(solution)/shard_map/reduce_scatter | solution.py:32
  276.6 1.1 multiply_reduce_fusion
  277.8 40.8 %psum.23 = f32[256]{0:T(256)S(1)} all-reduce(f32[256]{0:T(256)S(1)} %multiply_reduce_fusion), channel_id=1, replica_groups=mesh['col'=16,'row'=2] {'col','row'}, use_global_device_ids=true, to_apply=%region_8.9 | all-reduce | flops 256 | bytes 2048 | tf_op jit(solution)/shard_map/psum | solution.py:33
  318.6 1.9 broadcast_divide_fusion
  320.5 16.1 %multiply_convert_fusion = bf16[2048,1024]{1,0:T(8,128)(2,1)} fusion(f32[128,2048]{1,0:T(8,128)S(1)} %fusion.8, f32[128,2048]{1,0:T(8,128)S(1)} %fusion.2, f32[1024,256]{1,0:T(8,128)} %all-gather.5.cloned.1.call-done, f32[256]{0:T(256)S(1)} %add_sqrt_fusion), kind=kOutput, calls=%fused_computation.2 | convolution fusion | flops 6447431680 | bytes 7341056 | tf_op jit(solution)/shard_map/dot_general | solution.py:44
  336.6 18.4 %multiply_subtract_fusion = f32[2048,1024]{1,0:T(8,128)} fusion(f32[1024,256]{1,0:T(8,128)S(1)} %copy-done.3, f32[2048,1024]{1,0:T(8,128)} %param.4, bf16[2048,1024]{1,0:T(8,128)(2,1)S(1)} %copy-done.1, f32[128,2048]{1,0:T(8,128)S(1)} %fusion.8, f32[128,2048]{1,0:T(8,128)S(1)} %fusion.2), kind=kOutput, calls=%fused_computation.3 | convolution fusion | flops 6451363840 | bytes 24117248 | tf_op jit(solution)/shard_map/dot_general | solution.py:39
  (35 shorter events, 4.0 us)
Async XLA Ops:
  7.2 14.1 %all-gather.3.cloned.1.call-start = ((), (), s32[]{:S(2)}) async-start(), calls=%async_computation.1 | async-start | bytes 1572864 | tf_op jit(solution)/shard_map/all_gather | solution.py:17
  7.9 152.3 %all-reduce.4.cloned.1.call-start = ((), (), s32[]{:S(2)}) async-start(), calls=%async_computation.2 | async-start | bytes 4194304 | tf_op jit(solution)/shard_map/psum | solution.py:22
  32.3 152.1 %all-reduce.6.cloned.1.call-start = ((), (), s32[]{:S(2)}) async-start(), calls=%async_computation.3 | async-start | bytes 524288 | tf_op jit(solution)/shard_map/psum | solution.py:26
  160.2 86.0 %copy-start.2 = (f32[2048,256]{1,0:T(8,128)S(1)}, f32[2048,256]{1,0:T(8,128)}, u32[]{:S(2)}) copy-start(f32[2048,256]{1,0:T(8,128)} %all-reduce.4.cloned.1.call-done) | copy-start | bytes 6291460
  166.8 109.9 %reduce-scatter.2.cloned.1.call-start = ((), (), s32[]{:S(2)}) async-start(), calls=%async_computation.4 | async-start | bytes 1572864 | tf_op jit(solution)/shard_map/reduce_scatter | solution.py:32
  246.2 4.0 %copy-start = (bf16[2048,1024]{1,0:T(8,128)(2,1)S(1)}, bf16[2048,1024]{1,0:T(8,128)(2,1)}, u32[]{:S(2)}) copy-start(bf16[2048,1024]{1,0:T(8,128)(2,1)} %param.3) | copy-start | bytes 12582916
  266.9 53.6 %all-gather.5.cloned.1.call-start = ((), (), s32[]{:S(2)}) async-start(), calls=%async_computation.5 | async-start | bytes 1572864 | tf_op jit(solution)/shard_map/all_gather | solution.py:36
  320.5 16.1 %copy-start.1 = (bf16[2048,1024]{1,0:T(8,128)(2,1)S(1)}, bf16[2048,1024]{1,0:T(8,128)(2,1)}, u32[]{:S(2)}) copy-start(bf16[2048,1024]{1,0:T(8,128)(2,1)} %param.3) | copy-start | bytes 12582916
  320.5 16.1 %copy-start.3 = (f32[1024,256]{1,0:T(8,128)S(1)}, f32[1024,256]{1,0:T(8,128)}, u32[]{:S(2)}) copy-start(f32[1024,256]{1,0:T(8,128)} %all-gather.5.cloned.1.call-done) | copy-start | bytes 3145732
Sparse Core Ops, SparseCore 0:
  9.5 11.7 all-gather.2
  32.4 127.7 all-reduce.3
  166.9 17.4 all-reduce.5
  267.0 9.5 reduce-scatter.1
  278.0 10.2 all-gather.4
where the time goes:
time: 368 us; the launch traced here: 362 us
  waiting for transfers between devices  169 us (46%)
  matrix products  73.1 us (20%)
  other arithmetic  57.7 us (16%)
  blocking collectives  40.8 us (11%)
  between operations  15.5 us (4%)
  local copies, waits for them, and re-layouts  5.14 us (1%)
    psum x1, waiting for transfers between devices, body(): left = lax.psum(partial_value, 'col')  128 us
    psum x1, blocking collectives, body(): squares_right = lax.psum(jnp.sum(share * share, axis=0), ('col', 'row'))  40.8 us
    another operation x6, other arithmetic, body(): lower = jnp.linalg.cholesky(gram)  34 us
    another operation x3, other arithmetic, body(): left_orth = jax.scipy.linalg.solve_triangular(lower, left.T, lower=True).T  19.7 us
    dot_general x1, matrix products, body(): lax.dot_general(left_orth, right_whole, contract_cols, precision=highest,...  18.4 us
    psum x1, waiting for transfers between devices, body(): gram = lax.psum(local_gram, 'row')  17 us
    dot_general x1, matrix products, body(): lax.dot_general(blend, left_orth, contract_rows, precision=highest, prefe...  16.6 us
    dot_general x1, matrix products, body(): lax.dot_general(left_orth, right_unit, contract_cols, precision=highest,...  16.1 us
  transfers between devices with their start and end apart: 5, of which 4 were waited for; matrix products, arithmetic and copies ran while one was open for 1% of the time, Pallas kernels for 0%

commit v1 on v0

--- a/solution.py
+++ b/solution.py
@@ -30,7 +30,7 @@
         blend, left_orth, contract_rows, precision=highest, preferred_element_type=jnp.float32
     )
     share = lax.psum_scatter(right_local, "row", scatter_dimension=0, tiled=True)
-    squares_right = lax.psum(jnp.sum(share * share, axis=0), ("col", "row"))
+    squares_right = lax.psum(lax.psum(jnp.sum(share * share, axis=0), "row"), "col")
     right_norm = jnp.sqrt(squares_right + EPS)
     right_next = share / right_norm[None, :]
     right_whole = lax.all_gather(share, "row", axis=0, tiled=True)

time: 368 us -> 372 us (1.011)
  blocking collectives: 40.8 us -> 44.7 us
    psum x1 -> x2, blocking collectives: 40.8 us -> 44.7 us  [the longest x1 42.2 us: body(): lax.psum(lax.psum(jnp.sum(share * share, axis=0), 'row'), 'col')]
where the time goes in v1:
time: 372 us; the launch traced here: 366 us
  waiting for transfers between devices  169 us (45%)
  matrix products  73.1 us (20%)
  other arithmetic  57.7 us (16%)
  blocking collectives  44.7 us (12%)
  between operations  15.5 us (4%)
  local copies, waits for them, and re-layouts  5.14 us (1%)
    psum x1, waiting for transfers between devices, body(): left = lax.psum(partial_value, 'col')  128 us
    psum x1, blocking collectives, body(): lax.psum(lax.psum(jnp.sum(share * share, axis=0), 'row'), 'col')  42.2 us
    another operation x6, other arithmetic, body(): lower = jnp.linalg.cholesky(gram)  34 us
    another operation x3, other arithmetic, body(): left_orth = jax.scipy.linalg.solve_triangular(lower, left.T, lower=True).T  19.7 us
    dot_general x1, matrix products, body(): lax.dot_general(left_orth, right_whole, contract_cols, precision=highest,...  18.4 us
    psum x1, waiting for transfers between devices, body(): gram = lax.psum(local_gram, 'row')  17 us
    dot_general x1, matrix products, body(): lax.dot_general(blend, left_orth, contract_rows, precision=highest, prefe...  16.6 us
    dot_general x1, matrix products, body(): lax.dot_general(left_orth, right_unit, contract_cols, precision=highest,...  16.1 us
  transfers between devices with their start and end apart: 5, of which 4 were waited for; matrix products, arithmetic and copies ran while one was open for 1% of the time, Pallas kernels for 0%

profile of v1, /device:TPU:0, one launch (start us, length us, event | category | flops | bytes accessed | tf_op | source)
XLA Modules:
  0.0 365.7 jit_solution(13230017484694093963)
XLA Ops:
  7.9 13.4 %all-gather.3.cloned.1.call-done = f32[1024,256]{1,0:T(8,128)} async-done(((f32[512,256]{1,0:T(8,128)}), f32[1024,256]{1,0:T(8,128)}) %all-gather.3.cloned.1.call-update) | async-done | bytes 1048592 | tf_op jit(solution)/shard_map/all_gather | solution.py:17
  21.3 11.0 %fusion.1 = f32[2048,256]{1,0:T(8,128)} fusion(f32[1024,256]{1,0:T(8,128)} %all-gather.3.cloned.1.call-done, f32[2048,1024]{1,0:T(8,128)} %param.4, bf16[2048,1024]{1,0:T(8,128)(2,1)} %param.3), kind=kOutput, calls=%fused_computation.6 | convolution fusion | flops 6446645248 | bytes 15728640 | tf_op jit(solution)/shard_map/dot_general | solution.py:19
  32.3 127.9 %all-reduce.4.cloned.1.call-done = f32[2048,256]{1,0:T(8,128)} async-done(((f32[2048,256]{1,0:T(8,128)}), f32[2048,256]{1,0:T(8,128)}) %all-reduce.4.cloned.1.call-update) | async-done | bytes 2097168 | tf_op jit(solution)/shard_map/psum | solution.py:22
  160.2 6.5 %fusion.16 = f32[256,256]{0,1:T(8,128)} fusion(f32[2048,256]{1,0:T(8,128)} %all-reduce.4.cloned.1.call-done), kind=kOutput, calls=%fused_computation.42 | convolution fusion | flops 1610612736 | bytes 2359296 | tf_op jit(solution)/shard_map/dot_general | solution.py:23
  167.3 17.0 %all-reduce.6.cloned.1.call-done = f32[256,256]{0,1:T(8,128)} async-done(((f32[256,256]{0,1:T(8,128)}), f32[256,256]{0,1:T(8,128)}) %all-reduce.6.cloned.1.call-update) | async-done | bytes 262160 | tf_op jit(solution)/shard_map/psum | solution.py:26
  184.4 1.1 copy.7
  186.5 11.7 %cholesky.50 = f32[128,128]{1,0:T(8,128)S(1)} custom-call(f32[128,128]{1,0:T(8,128)S(1)} %cholesky.118), custom_call_target="Cholesky" | custom-call | tf_op jit(solution)/shard_map/jit(cholesky)/cholesky | solution.py:27
  198.2 9.8 %custom-call.15 = f32[1,128,128]{1,2,0:T(8,128)S(1)} custom-call(f32[1,128,128]{2,1,0:T(8,128)S(1)} %get-tuple-element.24), custom_call_target="InvertDiagBlocksLowerTriangular" | custom-call | tf_op jit(solution)/shard_map/jit(cholesky)/cholesky | solution.py:27
  208.5 11.7 %cholesky.105 = f32[128,128]{1,0:T(8,128)S(1)} custom-call(f32[128,128]{1,0:T(8,128)S(1)} %convolution_subtract_fusion.1), custom_call_target="Cholesky" | custom-call | tf_op jit(solution)/shard_map/jit(cholesky)/cholesky | solution.py:27
  222.3 4.2 %while.1 = (s32[]{:T(128)}, f32[256,256]{1,0:T(8,128)S(1)}, s32[2,2]{1,0:T(2,128)S(1)}, f32[2,128,128]{2,1,0:T(8,128)S(1)}, s32[]{:T(128)}) while((s32[]{:T(128)}, f32[256,256]{1,0:T(8,128)S(1)}, s32[2,2]{1,0:T(2,128)S(1)}, f32[2,128,128]{2,1,0:T(8,128)S(1)}, s32[]{:T(128)}) %tuple.27), condition=%wide.while_cond, body=%wide.while_body.sunk | while | flops 2 | bytes 131189 | solution.py:28
  223.1 1.4 bitcast_dynamic-update-slice_fusion.2
  225.1 1.4 bitcast_dynamic-update-slice_fusion.2
  226.5 19.7 %custom-call.16 = f32[2,128,128]{1,2,0:T(8,128)S(1)} custom-call(f32[2,128,128]{2,1,0:T(8,128)S(1)} %get-tuple-element.10), custom_call_target="InvertDiagBlocksLowerTriangular" | custom-call | tf_op jit(solution)/shard_map/jit(_solve_triangular)/triangular_solve | solution.py:28
  246.2 1.1 fusion.2
  247.3 1.8 convolution_subtract_fusion
  249.1 1.1 fusion.8
  250.2 16.6 %fusion = f32[1024,256]{1,0:T(8,128)} fusion(f32[2048,1024]{1,0:T(8,128)} %param.4, bf16[2048,1024]{1,0:T(8,128)(2,1)S(1)} %copy-done, f32[128,2048]{1,0:T(8,128)S(1)} %fusion.8, f32[128,2048]{1,0:T(8,128)S(1)} %fusion.2), kind=kOutput, calls=%fused_computation.5 | convolution fusion | flops 6447169536 | bytes 15728640 | tf_op jit(solution)/shard_map/dot_general | solution.py:29
  266.9 9.7 %reduce-scatter.2.cloned.1.call-done = f32[512,256]{1,0:T(8,128)} async-done(((f32[1024,256]{1,0:T(8,128)}), f32[512,256]{1,0:T(8,128)}) %reduce-scatter.2.cloned.1.call-update) | async-done | bytes 524304 | tf_op jit(solution)/shard_map/reduce_scatter | solution.py:32
  276.6 1.1 multiply_reduce_fusion
  277.8 2.5 psum.30
  280.2 42.2 %psum.31 = f32[256]{0:T(256)S(1)} all-reduce(f32[256]{0:T(256)S(1)} %psum.30), channel_id=1, replica_groups=mesh['col'=16,'row'=2] {'col'}, use_global_device_ids=true, to_apply=%region_9.10 | all-reduce | flops 256 | bytes 2048 | tf_op jit(solution)/shard_map/psum | solution.py:33
  322.5 1.9 broadcast_divide_fusion
  324.3 16.1 %multiply_convert_fusion = bf16[2048,1024]{1,0:T(8,128)(2,1)} fusion(f32[128,2048]{1,0:T(8,128)S(1)} %fusion.8, f32[128,2048]{1,0:T(8,128)S(1)} %fusion.2, f32[1024,256]{1,0:T(8,128)} %all-gather.5.cloned.1.call-done, f32[256]{0:T(256)S(1)} %add_sqrt_fusion), kind=kOutput, calls=%fused_computation.2 | convolution fusion | flops 6447431680 | bytes 7341056 | tf_op jit(solution)/shard_map/dot_general | solution.py:44
  340.5 18.4 %multiply_subtract_fusion = f32[2048,1024]{1,0:T(8,128)} fusion(f32[1024,256]{1,0:T(8,128)S(1)} %copy-done.3, f32[2048,1024]{1,0:T(8,128)} %param.4, bf16[2048,1024]{1,0:T(8,128)(2,1)S(1)} %copy-done.1, f32[128,2048]{1,0:T(8,128)S(1)} %fusion.8, f32[128,2048]{1,0:T(8,128)S(1)} %fusion.2), kind=kOutput, calls=%fused_computation.3 | convolution fusion | flops 6451363840 | bytes 24117248 | tf_op jit(solution)/shard_map/dot_general | solution.py:39
  (36 shorter events, 5.0 us)
Async XLA Ops:
  7.2 14.1 %all-gather.3.cloned.1.call-start = ((), (), s32[]{:S(2)}) async-start(), calls=%async_computation.1 | async-start | bytes 1572864 | tf_op jit(solution)/shard_map/all_gather | solution.py:17
  7.9 152.3 %all-reduce.4.cloned.1.call-start = ((), (), s32[]{:S(2)}) async-start(), calls=%async_computation.2 | async-start | bytes 4194304 | tf_op jit(solution)/shard_map/psum | solution.py:22
  32.3 152.1 %all-reduce.6.cloned.1.call-start = ((), (), s32[]{:S(2)}) async-start(), calls=%async_computation.3 | async-start | bytes 524288 | tf_op jit(solution)/shard_map/psum | solution.py:26
  160.2 86.0 %copy-start.2 = (f32[2048,256]{1,0:T(8,128)S(1)}, f32[2048,256]{1,0:T(8,128)}, u32[]{:S(2)}) copy-start(f32[2048,256]{1,0:T(8,128)} %all-reduce.4.cloned.1.call-done) | copy-start | bytes 6291460
  166.8 109.9 %reduce-scatter.2.cloned.1.call-start = ((), (), s32[]{:S(2)}) async-start(), calls=%async_computation.4 | async-start | bytes 1572864 | tf_op jit(solution)/shard_map/reduce_scatter | solution.py:32
  246.2 4.0 %copy-start = (bf16[2048,1024]{1,0:T(8,128)(2,1)S(1)}, bf16[2048,1024]{1,0:T(8,128)(2,1)}, u32[]{:S(2)}) copy-start(bf16[2048,1024]{1,0:T(8,128)(2,1)} %param.3) | copy-start | bytes 12582916
  266.9 57.5 %all-gather.5.cloned.1.call-start = ((), (), s32[]{:S(2)}) async-start(), calls=%async_computation.5 | async-start | bytes 1572864 | tf_op jit(solution)/shard_map/all_gather | solution.py:36
  324.3 16.1 %copy-start.1 = (bf16[2048,1024]{1,0:T(8,128)(2,1)S(1)}, bf16[2048,1024]{1,0:T(8,128)(2,1)}, u32[]{:S(2)}) copy-start(bf16[2048,1024]{1,0:T(8,128)(2,1)} %param.3) | copy-start | bytes 12582916
  324.3 16.1 %copy-start.3 = (f32[1024,256]{1,0:T(8,128)S(1)}, f32[1024,256]{1,0:T(8,128)}, u32[]{:S(2)}) copy-start(f32[1024,256]{1,0:T(8,128)} %all-gather.5.cloned.1.call-done) | copy-start | bytes 3145732
Sparse Core Ops, SparseCore 0:
  9.5 11.7 all-gather.2
  32.4 127.7 all-reduce.3
  166.9 17.4 all-reduce.5
  267.0 9.5 reduce-scatter.1
  278.0 10.2 all-gather.4
